TPU v7x, 256 devices: a whole 4x4x8 slice. The times are simulated.
256 devices in a mesh: rows: 64 (over z, y, core), cols: 4 (over x).
Axes of the slice: x: 4, y: 4, z: 8, core: 2. Of those that a mesh axis runs over, the one named last changes fastest.
Arguments:
- gradients: float32 [256, 128, 4096], P(None, 'rows', 'cols'), may hold values from -6 to 6
- momentum: float32 [256, 128, 4096], P(None, 'rows', 'cols'), may hold values from -6 to 6
- weights: float32 [256, 128, 4096], P(None, 'rows', 'cols'), may hold values from -0.1875 to 0.1875
Outputs:
- new_weights: float32 [256, 128, 4096], P(None, 'rows', 'cols')
- new_momentum: float32 [256, 128, 4096], P(None, 'rows', 'cols')
All inputs are finite; a program needn't handle non-finite values.
Results may differ from a plain program's by a relative error of at most 0.0003.
Values sent between devices are 32-bit elements.
A program may use at most 64 MiB of HBM per device.

v0:
```python
import jax
import jax.numpy as jnp
from jax import lax
from jax.sharding import PartitionSpec as P

ITERS = 4
hold_rate = 0.8
learn_rate = 0.8
decay_rate = 0.1


def local(gradients, momentum, weights):
    new_momentum = hold_rate * momentum + gradients
    moved = lax.all_to_all(new_momentum, "rows", split_axis=0, concat_axis=1, tiled=True)
    whole = lax.all_to_all(moved, "cols", split_axis=0, concat_axis=2, tiled=True)
    iterate = whole * lax.rsqrt(jnp.sum(whole * whole, axis=(1, 2), keepdims=True) + 1e-06)
    for step in range(ITERS):
        gram = jnp.einsum("mik,mjk->mij", iterate, iterate, precision=lax.Precision.HIGHEST)
        mixed = -4.775 * gram + 2.0315 * jnp.einsum(
            "mij,mjk->mik", gram, gram, precision=lax.Precision.HIGHEST
        )
        iterate = 3.4445 * iterate + jnp.einsum(
            "mij,mjk->mik", mixed, iterate, precision=lax.Precision.HIGHEST
        )
    iterate = lax.all_to_all(iterate, "cols", split_axis=2, concat_axis=0, tiled=True)
    back = lax.all_to_all(iterate, "rows", split_axis=1, concat_axis=0, tiled=True)
    new_weights = (1.0 - learn_rate * decay_rate) * weights - learn_rate * back
    return (new_weights, new_momentum)


def solution(mesh):
    placed = (P(None, "rows", "cols"), P(None, "rows", "cols"), P(None, "rows", "cols"))
    return jax.shard_map(
        local,
        mesh=mesh,
        in_specs=placed,
        out_specs=(P(None, "rows", "cols"), P(None, "rows", "cols")),
        check_vma=False,
    )
```

profile of v0, /device:TPU:8, one launch (start us, length us, event | category | flops | bytes accessed | tf_op | source)
XLA Modules:
  0.0 229.1 jit_solution(2761105436010172675)
XLA Ops:
  0.6 3.7 %multiply_add_fusion = f32[256,2,1024]{2,1,0:T(2,128)S(1)} fusion(f32[256,2,1024]{2,1,0:T(2,128)} %param.3, f32[256,2,1024]{2,1,0:T(2,128)} %param.4), kind=kLoop, calls=%fused_computation.11 | loop fusion | flops 1048576 | bytes 6291456 | tf_op jit(solution)/shard_map/add | solution.py:13
  4.3 0.0 copy-start
  4.3 63.1 %all_to_all.54 = f32[256,2,1024]{2,1,0:T(2,128)S(1)} all-to-all(f32[256,2,1024]{2,1,0:T(2,128)S(1)} %multiply_add_fusion), channel_id=1, replica_groups=mesh['rows'=64,'cols'=4] {'rows'}, dimensions={0} | all-to-all | bytes 4194304 | tf_op jit(solution)/shard_map/all_to_all | solution.py:14
  67.4 0.0 copy-done
  67.4 0.8 copy.32
  68.3 2.4 %all_to_all.43 = f32[4,128,1024]{2,1,0:T(8,128)} reshape(f32[4,64,2,1024]{3,2,1,0:T(2,128)S(1)} %bitcast.56) | data formatting | bytes 4194304 | tf_op jit(solution)/shard_map/all_to_all | solution.py:14
  70.7 29.1 %all_to_all.55 = f32[4,128,1024]{2,1,0:T(8,128)S(1)} all-to-all(f32[4,128,1024]{2,1,0:T(8,128)} %all_to_all.43), channel_id=1, replica_groups=mesh['rows'=64,'cols'=4] {'cols'}, dimensions={0} | all-to-all | bytes 4194304 | tf_op jit(solution)/shard_map/all_to_all | solution.py:15
  99.8 1.1 multiply_reduce_fusion
  101.6 1.8 fusion.4
  103.4 0.2 fusion.10
  103.6 2.6 %multiply_bitcast_fusion.1 = (f32[1,128,4,1024]{3,1,2,0:T(8,128)}, f32[1,128,4,1024]{3,1,2,0:T(8,128)}) fusion(f32[4,128,1024]{2,1,0:T(8,128)S(1)} %all_to_all.55, f32[]{:T(128)S(6)} %rsqrt.4), kind=kLoop, calls=%fused_computation.13 | loop fusion | flops 1048576 | bytes 6291460 | tf_op jit(solution)/shard_map/mul | solution.py:16
  106.2 1.9 copy.26
  108.1 2.9 %copy.25 = f32[1,128,4,1024]{1,3,2,0:T(8,128)} copy(f32[1,128,4,1024]{3,1,2,0:T(8,128)} %get-tuple-element.3) | data formatting | bytes 4194304 | tf_op jit(solution)/shard_map/mul | solution.py:22
  111.0 3.0 %copy.27 = f32[128,4096]{1,0:T(8,128)} copy(f32[128,4096]{0,1:T(8,128)} %bitcast.57) | data formatting | bytes 4194304 | tf_op jit(solution)/shard_map/mul | solution.py:22
  114.0 3.6 %convolution_add_fusion.3 = f32[128,4096]{1,0:T(8,128)S(1)} fusion(f32[128,4096]{1,0:T(8,128)} %copy.27, f32[128,128]{1,0:T(8,128)S(1)} %fusion.10, f32[128,4096]{0,1:T(8,128)S(1)} %bitcast.55), kind=kOutput, calls=%fused_computation.4 | convolution fusion | flops 805830656 | bytes 6356992 | tf_op jit(solution)/shard_map/mij,mjk->mik/dot_general | solution.py:22
  117.5 1.8 fusion.12
  119.3 0.2 fusion.9
  119.6 2.0 convolution_add_fusion.2
  121.6 1.8 fusion.13
  123.4 0.2 fusion.8
  123.6 2.0 convolution_add_fusion.1
  125.7 1.8 fusion.14
  127.5 0.2 fusion.7
  127.7 2.3 fusion
  130.0 3.7 %copy.28 = f32[1,128,4096]{1,0,2:T(1,128)} copy(f32[1,128,4096]{2,1,0:T(8,128)S(1)} %fusion) | data formatting | bytes 4194304 | tf_op jit(solution)/shard_map/add | solution.py:22
  133.7 27.5 %all_to_all.56 = f32[1,128,4096]{1,0,2:T(1,128)S(1)} all-to-all(f32[1,128,4096]{1,0,2:T(1,128)} %copy.28), channel_id=1, replica_groups=mesh['rows'=64,'cols'=4] {'cols'}, dimensions={2} | all-to-all | bytes 4194304 | tf_op jit(solution)/shard_map/all_to_all | solution.py:25
  161.2 2.0 copy.29
  163.1 60.5 %all_to_all.57 = f32[4,128,1024]{2,0,1:T(4,128)S(1)} all-to-all(f32[4,128,1024]{2,0,1:T(4,128)} %bitcast.59), channel_id=1, replica_groups=mesh['rows'=64,'cols'=4] {'rows'}, dimensions={1} | all-to-all | bytes 4194304 | tf_op jit(solution)/shard_map/all_to_all | solution.py:26
  223.7 0.6 broadcast_multiply_fusion
  224.2 0.0 copy-start.1
  224.3 1.9 copy.30
  226.2 2.9 %bitcast_subtract_fusion = f32[256,2,1024]{2,1,0:T(2,128)} fusion(f32[64,4,2,1024]{3,2,1,0:T(2,128)S(1)} %copy.30, f32[256,2,1024]{2,1,0:T(2,128)S(1)} %copy-done.1), kind=kLoop, calls=%fused_computation.7 | loop fusion | flops 1048576 | bytes 6291456 | tf_op jit(solution)/shard_map/sub | solution.py:27
  (1 shorter events, 0.0 us)
Async XLA Ops:
  4.3 63.2 %copy-start = (f32[256,2,1024]{2,1,0:T(2,128)}, f32[256,2,1024]{2,1,0:T(2,128)S(1)}, u32[]{:S(2)}) copy-start(f32[256,2,1024]{2,1,0:T(2,128)S(1)} %multiply_add_fusion) | copy-start | bytes 6291460
  224.2 2.0 copy-start.1
where the time goes:
time: 230 us; the launch traced here: 229 us
  blocking collectives  180 us (78%)
  local copies, waits for them, and re-layouts  18.6 us (8%)
  matrix products  17.9 us (8%)
  other arithmetic  10.8 us (5%)
    all_to_all x1, blocking collectives, local(): lax.all_to_all(new_momentum, 'rows', split_axis=0, concat_axis=1, tiled=T...  63.1 us
    all_to_all x1, blocking collectives, local(): lax.all_to_all(iterate, 'rows', split_axis=1, concat_axis=0, tiled=True)  60.5 us
    all_to_all x1, blocking collectives, local(): lax.all_to_all(moved, 'cols', split_axis=0, concat_axis=2, tiled=True)  29.1 us
    all_to_all x1, blocking collectives, local(): lax.all_to_all(iterate, 'cols', split_axis=2, concat_axis=0, tiled=True)  27.5 us
    dot_general x4, matrix products, local(): jnp.einsum('mij,mjk->mik', mixed, iterate, precision=lax.Precision.HIGHEST)  9.94 us
    dot_general x4, matrix products, local(): jnp.einsum('mik,mjk->mij', iterate, iterate, precision=lax.Precision.HIGH...  7.17 us
    mul x2, local copies, waits for them, and re-layouts, local(): 3.4445 * iterate  5.84 us

commit v1 on v0

--- a/solution.py
+++ b/solution.py
@@ -22,7 +22,10 @@
         iterate = 3.4445 * iterate + jnp.einsum(
             "mij,mjk->mik", mixed, iterate, precision=lax.Precision.HIGHEST
         )
-    iterate = lax.all_to_all(iterate, "cols", split_axis=2, concat_axis=0, tiled=True)
+    iterate = jnp.concatenate(
+        jax.lax.all_to_all(jnp.stack(jnp.split(iterate, jax.lax.psum(1, "cols"), 2)), "cols", 0, 0),
+        axis=0,
+    )
     back = lax.all_to_all(iterate, "rows", split_axis=1, concat_axis=0, tiled=True)
     new_weights = (1.0 - learn_rate * decay_rate) * weights - learn_rate * back
     return (new_weights, new_momentum)

time: 230 us -> 224 us (0.974)
  local copies, waits for them, and re-layouts: 18.6 us -> 14.5 us
    add x1 -> x0, local copies, waits for them, and re-layouts: 3.7 us -> none  [local(): 3.4445 * iterate]
where the time goes in v1:
time: 224 us
  blocking collectives  179 us (80%)
  matrix products  17.9 us (8%)
  local copies, waits for them, and re-layouts  14.5 us (6%)
  other arithmetic  11.1 us (5%)
    all_to_all x1, blocking collectives, local(): lax.all_to_all(new_momentum, 'rows', split_axis=0, concat_axis=1, tiled=T...  63.1 us
    all_to_all x1, blocking collectives, local(): lax.all_to_all(iterate, 'rows', split_axis=1, concat_axis=0, tiled=True)  60.3 us
    all_to_all x1, blocking collectives, local(): lax.all_to_all(moved, 'cols', split_axis=0, concat_axis=2, tiled=True)  29.1 us
    all_to_all x1, blocking collectives, local(): jax.lax.all_to_all(jnp.stack(jnp.split(iterate, jax.lax.psum(1, 'cols'),...  26.4 us
    dot_general x4, matrix products, local(): jnp.einsum('mij,mjk->mik', mixed, iterate, precision=lax.Precision.HIGHEST)  9.95 us
    dot_general x4, matrix products, local(): jnp.einsum('mik,mjk->mij', iterate, iterate, precision=lax.Precision.HIGH...  7.17 us
    mul x2, local copies, waits for them, and re-layouts, local(): 3.4445 * iterate  5.8 us

profile of v1, /device:TPU:8, one launch (start us, length us, event | category | flops | bytes accessed | tf_op | source)
XLA Modules:
  0.0 224.0 jit_solution(7043752736201725749)
XLA Ops:
  0.6 3.7 %multiply_add_fusion = f32[256,2,1024]{2,1,0:T(2,128)S(1)} fusion(f32[256,2,1024]{2,1,0:T(2,128)} %param.3, f32[256,2,1024]{2,1,0:T(2,128)} %param.4), kind=kLoop, calls=%fused_computation.12 | loop fusion | flops 1048576 | bytes 6291456 | tf_op jit(solution)/shard_map/add | solution.py:13
  4.3 0.0 copy-start
  4.3 63.1 %all_to_all.41 = f32[256,2,1024]{2,1,0:T(2,128)S(1)} all-to-all(f32[256,2,1024]{2,1,0:T(2,128)S(1)} %multiply_add_fusion), channel_id=1, replica_groups=mesh['rows'=64,'cols'=4] {'rows'}, dimensions={0} | all-to-all | bytes 4194304 | tf_op jit(solution)/shard_map/all_to_all | solution.py:14
  67.4 0.8 copy.19
  68.3 2.4 %all_to_all.33 = f32[4,128,1024]{2,1,0:T(8,128)} reshape(f32[4,64,2,1024]{3,2,1,0:T(2,128)S(1)} %bitcast.61) | data formatting | bytes 4194304 | tf_op jit(solution)/shard_map/all_to_all | solution.py:14
  70.7 29.1 %all_to_all.42 = f32[4,128,1024]{2,1,0:T(8,128)S(1)} all-to-all(f32[4,128,1024]{2,1,0:T(8,128)} %all_to_all.33), channel_id=1, replica_groups=mesh['rows'=64,'cols'=4] {'cols'}, dimensions={0} | all-to-all | bytes 4194304 | tf_op jit(solution)/shard_map/all_to_all | solution.py:15
  99.8 1.1 multiply_reduce_fusion
  101.6 1.8 fusion.4
  103.4 0.2 fusion.10
  103.6 2.6 %multiply_bitcast_fusion.1 = (f32[1,128,4,1024]{3,1,2,0:T(8,128)}, f32[1,128,4,1024]{3,1,2,0:T(8,128)}) fusion(f32[4,128,1024]{2,1,0:T(8,128)S(1)} %all_to_all.42, f32[]{:T(128)S(6)} %rsqrt.4), kind=kLoop, calls=%fused_computation.14 | loop fusion | flops 1048576 | bytes 6291460 | tf_op jit(solution)/shard_map/mul | solution.py:16
  106.2 1.9 copy.14
  108.1 2.9 %copy.13 = f32[1,128,4,1024]{1,3,2,0:T(8,128)} copy(f32[1,128,4,1024]{3,1,2,0:T(8,128)} %get-tuple-element.7) | data formatting | bytes 4194304 | tf_op jit(solution)/shard_map/mul | solution.py:22
  111.0 2.9 %copy.15 = f32[128,4096]{1,0:T(8,128)} copy(f32[128,4096]{0,1:T(8,128)} %bitcast.62) | data formatting | bytes 4194304 | tf_op jit(solution)/shard_map/mul | solution.py:22
  113.9 3.6 %convolution_add_fusion.3 = f32[128,4096]{1,0:T(8,128)S(1)} fusion(f32[128,4096]{1,0:T(8,128)} %copy.15, f32[128,128]{1,0:T(8,128)S(1)} %fusion.10, f32[128,4096]{0,1:T(8,128)S(1)} %bitcast.60), kind=kOutput, calls=%fused_computation.4 | convolution fusion | flops 805830656 | bytes 6356992 | tf_op jit(solution)/shard_map/mij,mjk->mik/dot_general | solution.py:22
  117.5 1.8 fusion.12
  119.3 0.2 fusion.9
  119.5 2.0 convolution_add_fusion.2
  121.6 1.8 fusion.13
  123.4 0.2 fusion.8
  123.6 2.0 convolution_add_fusion.1
  125.6 1.8 fusion.14
  127.4 0.2 fusion.7
  127.6 2.3 %fusion = f32[1,128,4096]{2,1,0:T(8,128)S(1)} fusion(f32[128,128]{1,0:T(8,128)S(1)} %fusion.7, f32[128,4096]{1,0:T(8,128)S(1)} %convolution_add_fusion.1), kind=kOutput, calls=%fused_computation.1 | convolution fusion | flops 806354944 | bytes 4259840 | tf_op jit(solution)/shard_map/mij,mjk->mik/dot_general | solution.py:22
  129.9 0.2 slice_bitcast_fusion.3
  130.2 0.2 pad_maximum_fusion
  130.4 26.4 %all_to_all.43 = f32[4,1,128,1024]{3,2,1,0:T(8,128)S(1)} all-to-all(f32[4,1,128,1024]{3,2,1,0:T(8,128)S(1)} %pad_maximum_fusion), channel_id=1, replica_groups=mesh['rows'=64,'cols'=4] {'cols'}, dimensions={0} | all-to-all | bytes 4194304 | tf_op jit(solution)/shard_map/all_to_all | solution.py:26
  156.8 1.4 copy.16
  158.2 60.3 %all_to_all.44 = f32[4,128,1024]{2,0,1:T(4,128)S(1)} all-to-all(f32[4,128,1024]{2,0,1:T(4,128)S(1)} %copy.16), channel_id=1, replica_groups=mesh['rows'=64,'cols'=4] {'rows'}, dimensions={1} | all-to-all | bytes 4194304 | tf_op jit(solution)/shard_map/all_to_all | solution.py:29
  218.5 0.6 broadcast_multiply_fusion
  219.1 0.0 copy-start.1
  219.1 1.9 copy.17
  221.1 2.9 %bitcast_subtract_fusion = f32[256,2,1024]{2,1,0:T(2,128)} fusion(f32[64,4,2,1024]{3,2,1,0:T(2,128)S(1)} %copy.17, f32[256,2,1024]{2,1,0:T(2,128)S(1)} %copy-done.1), kind=kLoop, calls=%fused_computation.8 | loop fusion | flops 1048576 | bytes 6291456 | tf_op jit(solution)/shard_map/sub | solution.py:30
  (2 shorter events, 0.0 us)
Async XLA Ops:
  4.3 63.2 %copy-start = (f32[256,2,1024]{2,1,0:T(2,128)}, f32[256,2,1024]{2,1,0:T(2,128)S(1)}, u32[]{:S(2)}) copy-start(f32[256,2,1024]{2,1,0:T(2,128)S(1)} %multiply_add_fusion) | copy-start | bytes 6291460
  219.1 2.0 copy-start.1
